TPU v7x, 32 devices: a whole 2x2x4 slice. The times are simulated.
32 devices in a mesh: layer: 8 (over z, x), rep: 4 (over y, core).
Axes of the slice: x: 2, y: 2, z: 4, core: 2. Of those that a mesh axis runs over, the one named last changes fastest.
Arguments:
- inverse_root: bfloat16 [64, 16, 128, 128], P('layer', 'rep'), may hold values from -0.625 to 0.625
- square_root: bfloat16 [64, 16, 128, 128], P('layer', 'rep'), may hold values from -0.625 to 0.625
- pattern: int32 [64, 16], P('layer', 'rep'), may hold values from 0 to 1, as said below
Outputs:
- inverse_next: bfloat16 [64, 16, 128, 128], P('layer', 'rep')
- square_next: bfloat16 [64, 16, 128, 128], P('layer', 'rep')
Inputs may be any that keep to these rules, and one draw needn't show every extreme that they name: 1 marks a tile of the common pattern. Slot 8 is 1 in every block row, and slot w of block row i is 0 where i - 8 + w lies outside 0 to 63.
All inputs are finite; a program needn't handle non-finite values.
Results may differ from a plain program's by a relative error of at most 0.018.
Values may be sent and summed in bfloat16 or wider, within the bound.
No kernel may reach another device: no remote copies, remote signals or barrier semaphores. Data moves between devices by JAX's collectives and lax.ppermute only.
A program may use at most 128 MiB of HBM per device.

v0:
```python
import jax
import jax.numpy as jnp
from jax import lax
from jax.sharding import PartitionSpec as P


def passed_along(block, axis, distance):
    devices = range(lax.axis_size(axis))
    route = [(i - distance, i) for i in devices if i - distance in devices]
    return lax.ppermute(block, axis, route)


def band_product(left_tiles, right_tiles):
    row_count = left_tiles.shape[0]
    slot_count = left_tiles.shape[1]
    groups = lax.axis_size("rep")
    band_slots = slot_count * groups
    half_band = band_slots // 2
    window_rows = row_count + slot_count - 1
    depth_rows = -(-half_band // row_count)
    offsets = list(range(depth_rows, 0, -1)) + list(range(-1, -depth_rows - 1, -1))
    shifted = [passed_along(right_tiles, "layer", shift_by) for shift_by in offsets]
    extended = jnp.concatenate(shifted[:depth_rows] + [right_tiles] + shifted[depth_rows:], axis=0)
    first_row = depth_rows * row_count - half_band
    row_index = (
        first_row
        + jnp.arange(groups, dtype=jnp.int32)[:, None] * slot_count
        + jnp.arange(window_rows, dtype=jnp.int32)[None, :]
    )
    outgoing = jnp.take(extended, row_index, axis=0)
    incoming = lax.all_to_all(outgoing, "rep", split_axis=0, concat_axis=2, tiled=True)[0]
    replica = lax.axis_index("rep")
    wide_span = band_slots + slot_count - 1
    tile_size = left_tiles.shape[2]
    summed = jnp.zeros((row_count, wide_span, tile_size, tile_size), jnp.float32)
    for local_slot in range(slot_count):
        product = jnp.einsum(
            "iab,ivbc->ivac",
            left_tiles[:, local_slot],
            incoming[local_slot : local_slot + row_count],
            preferred_element_type=jnp.float32,
        )
        summed = summed + jnp.pad(
            product, ((0, 0), (local_slot, slot_count - 1 - local_slot), (0, 0), (0, 0))
        )
    padded = jnp.pad(summed, ((0, 0), (band_slots, band_slots), (0, 0), (0, 0)))
    offset = band_slots + half_band - replica * slot_count
    partial_value = lax.dynamic_slice_in_dim(padded, offset, band_slots, axis=1)
    return lax.psum_scatter(
        partial_value.astype(jnp.bfloat16), "rep", scatter_dimension=1, tiled=True
    ).astype(jnp.float32)


def body(inverse_root, square_root, pattern):
    in_pattern = (pattern == 1)[:, :, None, None]
    inverse_kept = jnp.where(in_pattern, inverse_root, jnp.zeros_like(inverse_root))
    square_kept = jnp.where(in_pattern, square_root, jnp.zeros_like(square_root))
    intersection = jnp.where(in_pattern, band_product(inverse_kept, square_kept), jnp.float32(0.0))
    slot_count = pattern.shape[1]
    half_band = slot_count * lax.axis_size("rep") // 2
    slot_ids = lax.axis_index("rep") * slot_count + jnp.arange(slot_count, dtype=jnp.int32)
    diagonal = (slot_ids == half_band).astype(jnp.float32)
    identity = jnp.eye(inverse_root.shape[2], dtype=jnp.float32)
    update = jnp.where(
        in_pattern,
        1.5 * diagonal[None, :, None, None] * identity - 0.5 * intersection,
        jnp.float32(0.0),
    ).astype(jnp.bfloat16)
    square_next = jnp.where(in_pattern, band_product(square_kept, update), jnp.float32(0.0)).astype(
        jnp.bfloat16
    )
    inverse_next = jnp.where(
        in_pattern, band_product(update, inverse_kept), jnp.float32(0.0)
    ).astype(jnp.bfloat16)
    return (inverse_next, square_next)


def solution(mesh):
    placed = (P("layer", "rep", None, None), P("layer", "rep", None, None), P("layer", "rep"))
    return jax.shard_map(
        body,
        mesh=mesh,
        in_specs=placed,
        out_specs=(P("layer", "rep", None, None), P("layer", "rep", None, None)),
        check_vma=False,
    )
```

profile of v0, /device:TPU:0, one launch (start us, length us, event | category | flops | bytes accessed | tf_op | source)
XLA Modules:
  0.0 669.6 jit_solution(13496988569349193323)
XLA Ops:
  17.1 43.2 %collective-permute-done.2 = bf16[8,4,128,128]{3,2,0,1:T(8,128)(2,1)S(1)} collective-permute-done((bf16[8,4,128,128]{3,2,0,1:T(8,128)(2,1)S(1)}, bf16[8,4,128,128]{3,2,0,1:T(8,128)(2,1)S(1)}, u32[]{:S(2)}, u32[]{:S(2)}) %collective-permute-start.2) | collective-permute-done | bytes 1048608 | tf_op jit(solution)/shard_map/ppermute | solution.py:10
  79.5 64.6 %all-to-all-done.1 = bf16[4,11,4,128,128]{4,3,2,1,0:T(8,128)(2,1)} async-done(((bf16[4,11,4,128,128]{4,3,2,1,0:T(8,128)(2,1)}), bf16[4,11,4,128,128]{4,3,2,1,0:T(8,128)(2,1)}, u32[]{:S(2)}, u32[]{:S(2)}) %all-to-all-start.1) | async-done | bytes 5767200 | tf_op jit(solution)/shard_map/all_to_all | solution.py:31
  144.1 12.2 %fusion.66 = (bf16[1,8,4,4,128,128]{5,4,3,1,2,0:T(8,128)(2,1)}, bf16[1,8,4,4,128,128]{5,4,3,1,2,0:T(8,128)(2,1)}, bf16[1,8,4,4,128,128]{5,4,3,1,2,0:T(8,128)(2,1)}, bf16[1,8,4,4,128,128]{5,4,3,1,2,0:T(8,128)(2,1)}) fusion(bf16[1,11,4,4,128,128]{5,4,3,1,2,0:T(8,128)(2,1)} %bitcast.6), kind=kLoop, calls=%fused_computation.82 | loop fusion | bytes 33554432 | tf_op jit(solution)/shard_map/slice | solution.py:40
  156.3 6.5 copy.8
  162.8 6.6 copy.10
  169.4 6.8 %fusion.27 = f32[8,16,128,128]{3,2,0,1:T(8,128)} fusion(bf16[8,16,128,128]{2,3,1,0:T(8,128)(2,1)} %bitcast.105, bf16[8,4,128,128]{3,2,0,1:T(8,128)(2,1)S(1)} %copy-done.7), kind=kOutput, calls=%fused_computation.39 | convolution fusion | flops 536870912 | bytes 12845056 | tf_op jit(solution)/shard_map/iab,ivbc->ivac/dot_general | solution.py:37
  180.7 6.5 copy.12
  187.1 6.7 fusion.33
  193.8 6.5 copy.14
  204.9 7.8 %pad_add_fusion.2 = bf16[8,19,128,128]{3,2,0,1:T(8,128)(2,1)S(1)} fusion(f32[8,16,128,128]{3,2,0,1:T(8,128)S(1)} %fusion.36, f32[8,16,128,128]{3,2,0,1:T(8,128)S(1)} %copy-done.1, f32[8,16,128,128]{3,2,0,1:T(8,128)} %fusion.30, f32[8,16,128,128]{3,2,0,1:T(8,128)} %fusion.27), kind=kLoop, calls=%fused_computation.8 | loop fusion | flops 9961472 | bytes 38535168 | tf_op jit(solution)/shard_map/add | solution.py:43
  221.7 39.2 %reduce-scatter.4.cloned.1.call-done = bf16[8,4,128,128]{3,2,0,1:T(8,128)(2,1)} async-done(((bf16[8,16,128,128]{3,2,0,1:T(8,128)(2,1)}), bf16[8,4,128,128]{3,2,0,1:T(8,128)(2,1)}) %reduce-scatter.4.cloned.1.call-update) | async-done | bytes 1048592 | tf_op jit(solution)/shard_map/reduce_scatter | solution.py:49
  268.0 11.1 %collective-permute-start.5 = (bf16[8,4,128,128]{3,2,0,1:T(8,128)(2,1)}, bf16[8,4,128,128]{3,2,0,1:T(8,128)(2,1)}, u32[]{:S(2)}, u32[]{:S(2)}) collective-permute-start(bf16[8,4,128,128]{3,2,0,1:T(8,128)(2,1)} %select_convert_fusion.2), channel_id=1, source_target_pairs={{4,0},{8,4},{12,8},{16,12},{20,16},{24,20},{28,24},{5,1},{9,5},{13... | collective-permute-start | bytes 3145736 | tf_op jit(solution)/shard_map/ppermute | solution.py:10
  287.0 25.1 %collective-permute-done.4 = bf16[8,4,128,128]{3,2,0,1:T(8,128)(2,1)} collective-permute-done((bf16[8,4,128,128]{3,2,0,1:T(8,128)(2,1)}, bf16[8,4,128,128]{3,2,0,1:T(8,128)(2,1)}, u32[]{:S(2)}, u32[]{:S(2)}) %collective-permute-start.4) | collective-permute-done | bytes 1048608 | tf_op jit(solution)/shard_map/ppermute | solution.py:10
  319.0 9.8 %broadcast_select_fusion = (bf16[4,11,4,128,128]{4,3,2,1,0:T(8,128)(2,1)}, bf16[4,11,4,128,128]{4,3,2,1,0:T(8,128)(2,1)}) fusion(bf16[4,11,4,128,128]{4,3,2,1,0:T(8,128)(2,1)} %bitcast.100, pred[4,11]{1,0:T(4,128)(4,1)S(1)} %compare_and_fusion, bf16[4,11,4,128,128]{4,3,2,1,0:T(8,128)(2,1)} %bitcast.99), kind=kLoop, calls=%fused_computation.12 | loop fusion | flops 5767168 | bytes 23068716 | tf_op jit(solution)/shard_map/jit(_take)/select_n | solution.py:30
  328.8 68.9 %all_to_all.45 = bf16[4,11,4,128,128]{4,3,2,1,0:T(8,128)(2,1)S(1)} all-to-all(bf16[4,11,4,128,128]{4,3,2,1,0:T(8,128)(2,1)} %get-tuple-element.20), channel_id=1, replica_groups=mesh['layer'=8,'rep'=4] {'rep'}, dimensions={0} | all-to-all | bytes 11534336 | tf_op jit(solution)/shard_map/all_to_all | solution.py:31
  397.7 6.7 fusion.65
  404.4 6.5 copy.6
  410.8 6.7 %fusion.39 = f32[8,16,128,128]{3,2,0,1:T(8,128)} fusion(bf16[8,16,128,128]{2,3,1,0:T(8,128)(2,1)} %bitcast.110, bf16[8,4,128,128]{3,2,0,1:T(8,128)(2,1)} %select_convert_fusion.2), kind=kOutput, calls=%fused_computation.43 | convolution fusion | flops 536870912 | bytes 12845056 | tf_op jit(solution)/shard_map/iab,ivbc->ivac/dot_general | solution.py:37
  417.5 6.4 copy.17
  424.0 6.7 fusion.42
  430.7 6.4 copy.19
  437.1 6.7 %fusion.45 = f32[8,16,128,128]{3,2,0,1:T(8,128)} fusion(bf16[8,16,128,128]{2,3,1,0:T(8,128)(2,1)} %bitcast.112, bf16[8,4,128,128]{3,2,0,1:T(8,128)(2,1)} %select_convert_fusion.2), kind=kOutput, calls=%fused_computation.45 | convolution fusion | flops 536870912 | bytes 12845056 | tf_op jit(solution)/shard_map/iab,ivbc->ivac/dot_general | solution.py:37
  443.8 6.4 copy.21
  455.0 7.8 %pad_add_fusion.1 = bf16[8,19,128,128]{3,2,0,1:T(8,128)(2,1)S(1)} fusion(f32[8,16,128,128]{3,2,0,1:T(8,128)S(1)} %fusion.48, f32[8,16,128,128]{3,2,0,1:T(8,128)S(1)} %copy-done, f32[8,16,128,128]{3,2,0,1:T(8,128)} %fusion.42, f32[8,16,128,128]{3,2,0,1:T(8,128)} %fusion.39), kind=kLoop, calls=%fused_computation.7 | loop fusion | flops 9961472 | bytes 38535168 | tf_op jit(solution)/shard_map/add | solution.py:43
  465.9 91.4 %all_to_all.46 = bf16[4,11,4,128,128]{4,3,2,1,0:T(8,128)(2,1)S(1)} all-to-all(bf16[4,11,4,128,128]{4,3,2,1,0:T(8,128)(2,1)} %get-tuple-element.19), channel_id=1, replica_groups=mesh['layer'=8,'rep'=4] {'rep'}, dimensions={0} | all-to-all | bytes 11534336 | tf_op jit(solution)/shard_map/all_to_all | solution.py:31
  557.3 6.7 %fusion.64 = (bf16[1,8,4,4,128,128]{5,4,3,1,2,0:T(8,128)(2,1)}, bf16[1,8,4,4,128,128]{5,4,3,1,2,0:T(8,128)(2,1)}, bf16[1,8,4,4,128,128]{5,4,3,1,2,0:T(8,128)(2,1)}, bf16[1,8,4,4,128,128]{5,4,3,1,2,0:T(8,128)(2,1)}) fusion(bf16[1,11,4,4,128,128]{5,4,3,1,2,0:T(8,128)(2,1)S(1)} %bitcast.97), kind=kLoop, calls=%fused_computation.80 | loop fusion | bytes 33554432 | tf_op jit(solution)/shard_map/slice | solution.py:40
  564.0 6.5 copy.23
  570.5 6.4 copy.25
  577.0 6.5 copy.27
  583.5 6.5 copy.29
  597.1 6.7 fusion.60
  612.8 45.7 %reduce-scatter.8.cloned.1.call-done = bf16[8,4,128,128]{3,2,0,1:T(8,128)(2,1)} async-done(((bf16[8,16,128,128]{3,2,0,1:T(8,128)(2,1)}), bf16[8,4,128,128]{3,2,0,1:T(8,128)(2,1)}) %reduce-scatter.8.cloned.1.call-update) | async-done | bytes 1048592 | tf_op jit(solution)/shard_map/reduce_scatter | solution.py:49
  (68 shorter events, 97.1 us)
Async XLA Ops:
  10.6 49.7 %copy-start.5 = (bf16[8,4,128,128]{3,2,0,1:T(8,128)(2,1)}, bf16[8,4,128,128]{3,2,0,1:T(8,128)(2,1)S(1)}, u32[]{:S(2)}) copy-start(bf16[8,4,128,128]{3,2,0,1:T(8,128)(2,1)S(1)} %get-tuple-element.21) | copy-start | bytes 3145732
  10.6 49.7 %collective-permute-start.2 = (bf16[8,4,128,128]{3,2,0,1:T(8,128)(2,1)S(1)}, bf16[8,4,128,128]{3,2,0,1:T(8,128)(2,1)S(1)}, u32[]{:S(2)}, u32[]{:S(2)}) collective-permute-start(bf16[8,4,128,128]{3,2,0,1:T(8,128)(2,1)S(1)} %get-tuple-element.21), channel_id=1, source_target_pairs={{0,4},{4,8},{8,12},{12,16},{16,20},{20,24},{24,28},{1,5},{5,9},{9,... | collective-permute-start | bytes 3145736 | tf_op jit(solution)/shard_map/ppermute | solution.py:10
  15.5 45.8 %collective-permute-start.3 = (bf16[8,4,128,128]{3,2,0,1:T(8,128)(2,1)S(1)}, bf16[8,4,128,128]{3,2,0,1:T(8,128)(2,1)}, u32[]{:S(2)}, u32[]{:S(2)}) collective-permute-start(bf16[8,4,128,128]{3,2,0,1:T(8,128)(2,1)S(1)} %get-tuple-element.21), channel_id=1, source_target_pairs={{4,0},{8,4},{12,8},{16,12},{20,16},{24,20},{28,24},{5,1},{9,5},{13... | collective-permute-start | bytes 3145736 | tf_op jit(solution)/shard_map/ppermute | solution.py:10
  60.3 1.0 copy-start.9
  73.9 70.2 %all-to-all-start.1 = ((bf16[4,11,4,128,128]{4,3,2,1,0:T(8,128)(2,1)}), bf16[4,11,4,128,128]{4,3,2,1,0:T(8,128)(2,1)}, u32[]{:S(2)}, u32[]{:S(2)}) async-start(bf16[4,11,4,128,128]{4,3,2,1,0:T(8,128)(2,1)} %broadcast_select_fusion.1), calls=%async_computation.1 | async-start | bytes 11534336 | tf_op jit(solution)/shard_map/all_to_all | solution.py:31
  79.1 181.8 %reduce-scatter.4.cloned.1.call-start = ((), (), s32[]{:S(2)}) async-start(), calls=%async_computation.6 | async-start | bytes 5242880 | tf_op jit(solution)/shard_map/reduce_scatter | solution.py:49
  162.8 6.6 copy-start.7
  169.4 6.8 %copy-start.4 = (bf16[1,8,4,4,128,128]{4,5,3,2,1,0:T(8,128)(2,1)S(1)}, bf16[1,8,4,4,128,128]{4,5,3,2,1,0:T(8,128)(2,1)}, u32[]{:S(2)}) copy-start(bf16[1,8,4,4,128,128]{4,5,3,2,1,0:T(8,128)(2,1)} %copy.10) | copy-start | bytes 12582916
  200.3 4.6 copy-start.1
  215.8 397.1 %reduce-scatter.6.cloned.1.call-start = ((), (), s32[]{:S(2)}) async-start(), calls=%async_computation.7 | async-start | bytes 5242880 | tf_op jit(solution)/shard_map/reduce_scatter | solution.py:49
  215.8 63.3 %collective-permute-start = (bf16[8,4,128,128]{3,2,0,1:T(8,128)(2,1)S(1)}, bf16[8,4,128,128]{3,2,0,1:T(8,128)(2,1)S(1)}, u32[]{:S(2)}, u32[]{:S(2)}) collective-permute-start(bf16[8,4,128,128]{3,2,0,1:T(8,128)(2,1)S(1)} %copy-done.7), channel_id=1, source_target_pairs={{0,4},{4,8},{8,12},{12,16},{16,20},{20,24},{24,28},{1,5},{5,9},{9,... | collective-permute-start | bytes 3145736 | tf_op jit(solution)/shard_map/ppermute | solution.py:10
  220.3 59.9 %collective-permute-start.1 = (bf16[8,4,128,128]{3,2,0,1:T(8,128)(2,1)S(1)}, bf16[8,4,128,128]{3,2,0,1:T(8,128)(2,1)}, u32[]{:S(2)}, u32[]{:S(2)}) collective-permute-start(bf16[8,4,128,128]{3,2,0,1:T(8,128)(2,1)S(1)} %copy-done.7), channel_id=1, source_target_pairs={{4,0},{8,4},{12,8},{16,12},{20,16},{24,20},{28,24},{5,1},{9,5},{13... | collective-permute-start | bytes 3145736 | tf_op jit(solution)/shard_map/ppermute | solution.py:10
  263.7 48.4 %collective-permute-start.4 = (bf16[8,4,128,128]{3,2,0,1:T(8,128)(2,1)}, bf16[8,4,128,128]{3,2,0,1:T(8,128)(2,1)}, u32[]{:S(2)}, u32[]{:S(2)}) collective-permute-start(bf16[8,4,128,128]{3,2,0,1:T(8,128)(2,1)} %select_convert_fusion.2), channel_id=1, source_target_pairs={{0,4},{4,8},{8,12},{12,16},{16,20},{20,24},{24,28},{1,5},{5,9},{9,... | collective-permute-start | bytes 3145736 | tf_op jit(solution)/shard_map/ppermute | solution.py:10
  268.0 44.0 %collective-permute-start.5 = (bf16[8,4,128,128]{3,2,0,1:T(8,128)(2,1)}, bf16[8,4,128,128]{3,2,0,1:T(8,128)(2,1)}, u32[]{:S(2)}, u32[]{:S(2)}) collective-permute-start(bf16[8,4,128,128]{3,2,0,1:T(8,128)(2,1)} %select_convert_fusion.2), channel_id=1, source_target_pairs={{4,0},{8,4},{12,8},{16,12},{20,16},{24,20},{28,24},{5,1},{9,5},{13... | collective-permute-start | bytes 3145736 | tf_op jit(solution)/shard_map/ppermute | solution.py:10
  279.2 1.0 copy-start.8
  450.3 4.7 copy-start
  465.9 192.7 %reduce-scatter.8.cloned.1.call-start = ((), (), s32[]{:S(2)}) async-start(), calls=%async_computation.8 | async-start | bytes 5242880 | tf_op jit(solution)/shard_map/reduce_scatter | solution.py:49
  583.5 6.5 copy-start.6
  590.0 3.6 copy-start.2
  593.6 2.2 copy-start.3
Sparse Core Ops, SparseCore 0:
  215.9 44.9 reduce-scatter.3
  466.0 68.1 reduce-scatter.5
  612.9 45.5 reduce-scatter.7
where the time goes:
time: 675 us; the launch traced here: 670 us
  waiting for transfers between devices  218 us (32%)
  blocking collectives  160 us (24%)
  local copies, waits for them, and re-layouts  134 us (20%)
  matrix products  58.1 us (9%)
  other arithmetic  51.9 us (8%)
  starting transfers between devices  33.1 us (5%)
  between operations  14.2 us (2%)
    all_to_all x2, blocking collectives, band_product(): lax.all_to_all(outgoing, 'rep', split_axis=0, concat_axis=2, tiled=True)[0]  160 us
    slice x15, local copies, waits for them, and re-layouts, band_product(): incoming[local_slot:local_slot + row_count]  103 us
    reduce_scatter x3, waiting for transfers between devices, band_product(): lax.psum_scatter(partial_value.astype(jnp.bfloat16), 'rep', scatter_dimen...  84.9 us
    ppermute x6, waiting for transfers between devices, passed_along(): return lax.ppermute(block, axis, route)  68.3 us
    all_to_all x1, waiting for transfers between devices, band_product(): lax.all_to_all(outgoing, 'rep', split_axis=0, concat_axis=2, tiled=True)[0]  64.6 us
    dot_general x12, matrix products, band_product(): jnp.einsum('iab,ivbc->ivac', left_tiles[:, local_slot], incoming[local_sl...  58.1 us
    ppermute x6, starting transfers between devices, passed_along(): return lax.ppermute(block, axis, route)  27.4 us
    add x3, other arithmetic, band_product(): summed + jnp.pad(product, ((0, 0), (local_slot, slot_count - 1 - local_sl...  21.5 us
  transfers between devices with their start and end apart: 10, of which 5 were waited for; matrix products, arithmetic and copies ran while one was open for 10% of the time, Pallas kernels for 0%

commit v1 on v0

--- a/solution.py
+++ b/solution.py
@@ -2,6 +2,13 @@
 import jax.numpy as jnp
 from jax import lax
 from jax.sharding import PartitionSpec as P
+
+
+def stacked_exchange(x, axis, split, join):
+    size = lax.axis_size(axis)
+    blocks = jnp.stack(jnp.split(x, size, axis=split), axis=0)
+    blocks = lax.all_to_all(blocks, axis, split_axis=0, concat_axis=0)
+    return jnp.concatenate(blocks, axis=join)
 
 
 def passed_along(block, axis, distance):
@@ -28,7 +35,7 @@
         + jnp.arange(window_rows, dtype=jnp.int32)[None, :]
     )
     outgoing = jnp.take(extended, row_index, axis=0)
-    incoming = lax.all_to_all(outgoing, "rep", split_axis=0, concat_axis=2, tiled=True)[0]
+    incoming = stacked_exchange(outgoing, "rep", 0, 2)[0]
     replica = lax.axis_index("rep")
     wide_span = band_slots + slot_count - 1
     tile_size = left_tiles.shape[2]

time: 675 us -> 687 us (1.018)
  local copies, waits for them, and re-layouts: 134 us -> 143 us
    another operation x0 -> x2, local copies, waits for them, and re-layouts: none -> 8.24 us  [stacked_exchange(): blocks = jnp.stack(jnp.split(x, size, axis=split), axis=0)]
    another operation x0 -> x3, other arithmetic: none -> 8.18 us  [stacked_exchange(): blocks = jnp.stack(jnp.split(x, size, axis=split), axis=0)]
where the time goes in v1:
time: 687 us; the launch traced here: 681 us
  waiting for transfers between devices  216 us (31%)
  blocking collectives  158 us (23%)
  local copies, waits for them, and re-layouts  143 us (21%)
  matrix products  58.2 us (8%)
  other arithmetic  57.4 us (8%)
  starting transfers between devices  34.6 us (5%)
  between operations  14.2 us (2%)
    all_to_all x2, blocking collectives, stacked_exchange(): blocks = lax.all_to_all(blocks, axis, split_axis=0, concat_axis=0)  158 us
    slice x15, local copies, waits for them, and re-layouts, band_product(): incoming[local_slot:local_slot + row_count]  104 us
    reduce_scatter x3, waiting for transfers between devices, band_product(): lax.psum_scatter(partial_value.astype(jnp.bfloat16), 'rep', scatter_dimen...  84.9 us
    ppermute x6, waiting for transfers between devices, passed_along(): return lax.ppermute(block, axis, route)  66.8 us
    all_to_all x1, waiting for transfers between devices, stacked_exchange(): blocks = lax.all_to_all(blocks, axis, split_axis=0, concat_axis=0)  64.6 us
    dot_general x12, matrix products, band_product(): jnp.einsum('iab,ivbc->ivac', left_tiles[:, local_slot], incoming[local_sl...  58.2 us
    ppermute x6, starting transfers between devices, passed_along(): return lax.ppermute(block, axis, route)  29 us
    add x3, other arithmetic, band_product(): summed + jnp.pad(product, ((0, 0), (local_slot, slot_count - 1 - local_sl...  21.5 us
  transfers between devices with their start and end apart: 10, of which 5 were waited for; matrix products, arithmetic and copies ran while one was open for 10% of the time, Pallas kernels for 0%

profile of v1, /device:TPU:0, one launch (start us, length us, event | category | flops | bytes accessed | tf_op | source)
XLA Modules:
  0.0 681.2 jit_solution(265449950599985239)
XLA Ops:
  17.1 43.2 %collective-permute-done.2 = bf16[8,4,128,128]{3,2,0,1:T(8,128)(2,1)S(1)} collective-permute-done((bf16[8,4,128,128]{3,2,0,1:T(8,128)(2,1)S(1)}, bf16[8,4,128,128]{3,2,0,1:T(8,128)(2,1)S(1)}, u32[]{:S(2)}, u32[]{:S(2)}) %collective-permute-start.2) | collective-permute-done | bytes 1048608 | tf_op jit(solution)/shard_map/ppermute | solution.py:17
  81.6 64.6 %all-to-all-done.1 = bf16[4,1,11,4,128,128]{5,4,3,2,1,0:T(8,128)(2,1)} async-done(((bf16[4,1,11,4,128,128]{5,4,3,2,1,0:T(8,128)(2,1)}), bf16[4,1,11,4,128,128]{5,4,3,2,1,0:T(8,128)(2,1)}, u32[]{:S(2)}, u32[]{:S(2)}) %all-to-all-start.1) | async-done | bytes 5767200 | tf_op jit(solution)/shard_map/all_to_all | solution.py:10
  146.2 12.2 %fusion.66 = (bf16[1,8,4,4,128,128]{5,4,3,1,0,2:T(8,128)(2,1)}, bf16[1,8,4,4,128,128]{5,4,3,1,0,2:T(8,128)(2,1)}, bf16[1,8,4,4,128,128]{5,4,3,1,0,2:T(8,128)(2,1)}, bf16[1,8,4,4,128,128]{5,4,3,1,0,2:T(8,128)(2,1)}) fusion(bf16[1,11,4,4,128,128]{5,4,3,1,0,2:T(8,128)(2,1)} %bitcast.12), kind=kLoop, calls=%fused_computation.97 | loop fusion | bytes 33554432 | tf_op jit(solution)/shard_map/slice | solution.py:47
  158.4 6.5 copy.8
  164.9 6.6 copy.10
  171.5 6.9 %fusion.27 = f32[8,16,128,128]{3,2,0,1:T(8,128)} fusion(bf16[8,16,128,128]{2,3,1,0:T(8,128)(2,1)} %bitcast.123, bf16[8,4,128,128]{3,2,0,1:T(8,128)(2,1)S(1)} %copy-done.7), kind=kOutput, calls=%fused_computation.42 | convolution fusion | flops 536870912 | bytes 12845056 | tf_op jit(solution)/shard_map/iab,ivbc->ivac/dot_general | solution.py:44
  182.8 6.5 copy.12
  189.3 6.7 fusion.33
  196.1 6.5 copy.14
  207.2 7.8 %pad_add_fusion.2 = bf16[8,19,128,128]{3,2,0,1:T(8,128)(2,1)S(1)} fusion(f32[8,16,128,128]{3,2,0,1:T(8,128)S(1)} %fusion.36, f32[8,16,128,128]{3,2,0,1:T(8,128)S(1)} %copy-done.1, f32[8,16,128,128]{3,2,0,1:T(8,128)} %fusion.30, f32[8,16,128,128]{3,2,0,1:T(8,128)} %fusion.27), kind=kLoop, calls=%fused_computation.8 | loop fusion | flops 9961472 | bytes 38535168 | tf_op jit(solution)/shard_map/add | solution.py:50
  224.0 39.2 %reduce-scatter.4.cloned.1.call-done = bf16[8,4,128,128]{3,2,0,1:T(8,128)(2,1)} async-done(((bf16[8,16,128,128]{3,2,0,1:T(8,128)(2,1)}), bf16[8,4,128,128]{3,2,0,1:T(8,128)(2,1)}) %reduce-scatter.4.cloned.1.call-update) | async-done | bytes 1048592 | tf_op jit(solution)/shard_map/reduce_scatter | solution.py:56
  270.3 12.7 %collective-permute-start.5 = (bf16[8,4,128,128]{3,2,0,1:T(8,128)(2,1)}, bf16[8,4,128,128]{3,2,0,1:T(8,128)(2,1)}, u32[]{:S(2)}, u32[]{:S(2)}) collective-permute-start(bf16[8,4,128,128]{3,2,0,1:T(8,128)(2,1)} %select_convert_fusion.2), channel_id=1, source_target_pairs={{4,0},{8,4},{12,8},{16,12},{20,16},{24,20},{28,24},{5,1},{9,5},{13... | collective-permute-start | bytes 3145736 | tf_op jit(solution)/shard_map/ppermute | solution.py:17
  290.9 23.5 %collective-permute-done.4 = bf16[8,4,128,128]{3,2,0,1:T(8,128)(2,1)} collective-permute-done((bf16[8,4,128,128]{3,2,0,1:T(8,128)(2,1)}, bf16[8,4,128,128]{3,2,0,1:T(8,128)(2,1)}, u32[]{:S(2)}, u32[]{:S(2)}) %collective-permute-start.4) | collective-permute-done | bytes 1048608 | tf_op jit(solution)/shard_map/ppermute | solution.py:17
  321.2 9.6 %broadcast_select_fusion = (bf16[4,11,4,128,128]{4,3,2,1,0:T(8,128)(2,1)}, bf16[4,11,4,128,128]{4,3,2,1,0:T(8,128)(2,1)}) fusion(bf16[4,11,4,128,128]{4,3,2,1,0:T(8,128)(2,1)} %bitcast.118, pred[4,11]{1,0:T(4,128)(4,1)S(1)} %compare_and_fusion, bf16[4,11,4,128,128]{4,3,2,1,0:T(8,128)(2,1)} %bitcast.117), kind=kLoop, calls=%fused_computation.15 | loop fusion | flops 5767168 | bytes 23068716 | tf_op jit(solution)/shard_map/jit(_take)/select_n | solution.py:37
  330.8 7.0 %slice_bitcast_fusion.3 = (bf16[1,1,11,4,128,128]{5,4,3,2,1,0:T(8,128)(2,1)S(1)}, bf16[1,1,11,4,128,128]{5,4,3,2,1,0:T(8,128)(2,1)S(1)}, bf16[1,1,11,4,128,128]{...) fusion(bf16[4,11,4,128,128]{4,3,2,1,0:T(8,128)(2,1)} %get-tuple, ...), kind=kLoop, calls=%fused_computation.63 | loop fusion | bytes 23068672 | tf_op jit(solution)/shard_map/stack | solution.py:9
  339.4 67.6 %all_to_all.15 = bf16[4,1,11,4,128,128]{5,4,3,2,1,0:T(8,128)(2,1)S(1)} all-to-all(bf16[4,1,11,4,128,128]{5,4,3,2,1,0:T(8,128)(2,1)S(1)} %pad_maximum_fusion), channel_id=1, replica_groups=mesh['layer'=8,'rep'=4] {'rep'}, dimensions={0} | all-to-all | bytes 11534336 | tf_op jit(solution)/shard_map/all_to_all | solution.py:10
  407.0 6.7 fusion.65
  413.7 6.4 copy.6
  420.1 6.7 fusion.39
  426.9 6.5 copy.17
  433.4 6.7 fusion.42
  440.1 6.5 copy.19
  446.6 6.7 fusion.45
  453.3 6.5 copy.21
  464.5 7.8 %pad_add_fusion.1 = bf16[8,19,128,128]{3,2,0,1:T(8,128)(2,1)S(1)} fusion(f32[8,16,128,128]{3,2,0,1:T(8,128)S(1)} %fusion.48, f32[8,16,128,128]{3,2,0,1:T(8,128)S(1)} %copy-done, f32[8,16,128,128]{3,2,0,1:T(8,128)} %fusion.42, f32[8,16,128,128]{3,2,0,1:T(8,128)} %fusion.39), kind=kLoop, calls=%fused_computation.7 | loop fusion | flops 9961472 | bytes 38535168 | tf_op jit(solution)/shard_map/add | solution.py:50
  478.8 90.1 %all_to_all.16 = bf16[4,1,11,4,128,128]{5,4,3,2,1,0:T(8,128)(2,1)S(1)} all-to-all(bf16[4,1,11,4,128,128]{5,4,3,2,1,0:T(8,128)(2,1)S(1)} %pad_maximum_fusion.2), channel_id=1, replica_groups=mesh['layer'=8,'rep'=4] {'rep'}, dimensions={0} | all-to-all | bytes 11534336 | tf_op jit(solution)/shard_map/all_to_all | solution.py:10
  568.9 6.7 fusion.64
  575.6 6.5 copy.23
  588.5 6.5 copy.27
  595.0 6.5 copy.29
  608.6 6.7 fusion.60
  624.4 45.7 %reduce-scatter.8.cloned.1.call-done = bf16[8,4,128,128]{3,2,0,1:T(8,128)(2,1)} async-done(((bf16[8,16,128,128]{3,2,0,1:T(8,128)(2,1)}), bf16[8,4,128,128]{3,2,0,1:T(8,128)(2,1)}) %reduce-scatter.8.cloned.1.call-update) | async-done | bytes 1048592 | tf_op jit(solution)/shard_map/reduce_scatter | solution.py:56
  (73 shorter events, 110.5 us)
Async XLA Ops:
  10.6 49.7 %copy-start.5 = (bf16[8,4,128,128]{3,2,0,1:T(8,128)(2,1)}, bf16[8,4,128,128]{3,2,0,1:T(8,128)(2,1)S(1)}, u32[]{:S(2)}) copy-start(bf16[8,4,128,128]{3,2,0,1:T(8,128)(2,1)S(1)} %get-tuple-element.33) | copy-start | bytes 3145732
  10.6 49.7 %collective-permute-start.2 = (bf16[8,4,128,128]{3,2,0,1:T(8,128)(2,1)S(1)}, bf16[8,4,128,128]{3,2,0,1:T(8,128)(2,1)S(1)}, u32[]{:S(2)}, u32[]{:S(2)}) collective-permute-start(bf16[8,4,128,128]{3,2,0,1:T(8,128)(2,1)S(1)} %get-tuple-element.33), channel_id=1, source_target_pairs={{0,4},{4,8},{8,12},{12,16},{16,20},{20,24},{24,28},{1,5},{5,9},{9,... | collective-permute-start | bytes 3145736 | tf_op jit(solution)/shard_map/ppermute | solution.py:17
  15.5 45.8 %collective-permute-start.3 = (bf16[8,4,128,128]{3,2,0,1:T(8,128)(2,1)S(1)}, bf16[8,4,128,128]{3,2,0,1:T(8,128)(2,1)}, u32[]{:S(2)}, u32[]{:S(2)}) collective-permute-start(bf16[8,4,128,128]{3,2,0,1:T(8,128)(2,1)S(1)} %get-tuple-element.33), channel_id=1, source_target_pairs={{4,0},{8,4},{12,8},{16,12},{20,16},{24,20},{28,24},{5,1},{9,5},{13... | collective-permute-start | bytes 3145736 | tf_op jit(solution)/shard_map/ppermute | solution.py:17
  60.3 1.0 copy-start.9
  76.0 70.2 %all-to-all-start.1 = ((bf16[4,1,11,4,128,128]{5,4,3,2,1,0:T(8,128)(2,1)}), bf16[4,1,11,4,128,128]{5,4,3,2,1,0:T(8,128)(2,1)}, u32[]{:S(2)}, u32[]{:S(2)}) async-start(bf16[4,1,11,4,128,128]{5,4,3,2,1,0:T(8,128)(2,1)} %pad_maximum_fusion.1), calls=%async_computation.1 | async-start | bytes 11534336 | tf_op jit(solution)/shard_map/all_to_all | solution.py:10
  81.1 182.0 %reduce-scatter.4.cloned.1.call-start = ((), (), s32[]{:S(2)}) async-start(), calls=%async_computation.6 | async-start | bytes 5242880 | tf_op jit(solution)/shard_map/reduce_scatter | solution.py:56
  164.9 6.6 copy-start.7
  171.5 6.9 %copy-start.4 = (bf16[1,8,4,4,128,128]{4,5,3,2,1,0:T(8,128)(2,1)S(1)}, bf16[1,8,4,4,128,128]{4,5,3,2,1,0:T(8,128)(2,1)}, u32[]{:S(2)}) copy-start(bf16[1,8,4,4,128,128]{4,5,3,2,1,0:T(8,128)(2,1)} %copy.10) | copy-start | bytes 12582916
  202.6 4.6 copy-start.1
  218.0 406.4 %reduce-scatter.6.cloned.1.call-start = ((), (), s32[]{:S(2)}) async-start(), calls=%async_computation.7 | async-start | bytes 5242880 | tf_op jit(solution)/shard_map/reduce_scatter | solution.py:56
  218.1 64.9 %collective-permute-start = (bf16[8,4,128,128]{3,2,0,1:T(8,128)(2,1)S(1)}, bf16[8,4,128,128]{3,2,0,1:T(8,128)(2,1)S(1)}, u32[]{:S(2)}, u32[]{:S(2)}) collective-permute-start(bf16[8,4,128,128]{3,2,0,1:T(8,128)(2,1)S(1)} %copy-done.7), channel_id=1, source_target_pairs={{0,4},{4,8},{8,12},{12,16},{16,20},{20,24},{24,28},{1,5},{5,9},{9,... | collective-permute-start | bytes 3145736 | tf_op jit(solution)/shard_map/ppermute | solution.py:17
  222.5 61.5 %collective-permute-start.1 = (bf16[8,4,128,128]{3,2,0,1:T(8,128)(2,1)S(1)}, bf16[8,4,128,128]{3,2,0,1:T(8,128)(2,1)}, u32[]{:S(2)}, u32[]{:S(2)}) collective-permute-start(bf16[8,4,128,128]{3,2,0,1:T(8,128)(2,1)S(1)} %copy-done.7), channel_id=1, source_target_pairs={{4,0},{8,4},{12,8},{16,12},{20,16},{24,20},{28,24},{5,1},{9,5},{13... | collective-permute-start | bytes 3145736 | tf_op jit(solution)/shard_map/ppermute | solution.py:17
  266.0 48.4 %collective-permute-start.4 = (bf16[8,4,128,128]{3,2,0,1:T(8,128)(2,1)}, bf16[8,4,128,128]{3,2,0,1:T(8,128)(2,1)}, u32[]{:S(2)}, u32[]{:S(2)}) collective-permute-start(bf16[8,4,128,128]{3,2,0,1:T(8,128)(2,1)} %select_convert_fusion.2), channel_id=1, source_target_pairs={{0,4},{4,8},{8,12},{12,16},{16,20},{20,24},{24,28},{1,5},{5,9},{9,... | collective-permute-start | bytes 3145736 | tf_op jit(solution)/shard_map/ppermute | solution.py:17
  270.3 44.0 %collective-permute-start.5 = (bf16[8,4,128,128]{3,2,0,1:T(8,128)(2,1)}, bf16[8,4,128,128]{3,2,0,1:T(8,128)(2,1)}, u32[]{:S(2)}, u32[]{:S(2)}) collective-permute-start(bf16[8,4,128,128]{3,2,0,1:T(8,128)(2,1)} %select_convert_fusion.2), channel_id=1, source_target_pairs={{4,0},{8,4},{12,8},{16,12},{20,16},{24,20},{28,24},{5,1},{9,5},{13... | collective-permute-start | bytes 3145736 | tf_op jit(solution)/shard_map/ppermute | solution.py:17
  283.0 1.0 copy-start.8
  459.8 4.7 copy-start
  475.4 194.7 %reduce-scatter.8.cloned.1.call-start = ((), (), s32[]{:S(2)}) async-start(), calls=%async_computation.8 | async-start | bytes 5242880 | tf_op jit(solution)/shard_map/reduce_scatter | solution.py:56
  595.0 6.5 copy-start.6
  601.6 3.6 copy-start.2
  605.2 2.2 copy-start.3
Sparse Core Ops, SparseCore 0:
  218.2 44.9 reduce-scatter.3
  475.5 68.6 reduce-scatter.5
  624.5 45.5 reduce-scatter.7
